TPU v7x, 16 devices: a whole 2x2x2 slice. The times are simulated.
16 devices in a mesh: dp: 4 (over z, y), tp: 4 (over x, core).
Axes of the slice: x: 2, y: 2, z: 2, core: 2. Of those that a mesh axis runs over, the one named last changes fastest.
Arguments:
- enc_out: bfloat16 [32, 512, 4096], P('dp', 'tp'), parts along dimension 0
- norm_scale: bfloat16 [4096], replicated
- w_key: bfloat16 [4, 4096, 64, 64], P(None, None, 'tp')
- w_value: bfloat16 [4, 4096, 64, 64], P(None, None, 'tp')
Outputs:
- output 1: bfloat16 [4, 32, 512, 64, 64], P(None, 'dp', None, 'tp'), parts along dimension 1
- output 2: bfloat16 [4, 32, 512, 64, 64], P(None, 'dp', None, 'tp'), parts along dimension 1
There are 4 independent parts. A program takes and returns all parts, laid end to end along the dimension named above; an argument that names none is the same for every part.
All inputs are finite; a program needn't handle non-finite values.
Results may differ from a plain program's by a relative error of at most 0.001.
Values are sent between devices in bfloat16 or wider.
A program may use at most 1 GiB of HBM per device.

v0:
```python
import jax
import jax.numpy as jnp
from jax import lax
from jax.sharding import PartitionSpec as P

NORM_EPS = 1e-6


def rms_norm(enc_out, norm_scale):
    acts = enc_out.astype(jnp.float32)
    mean_sq = jnp.mean(acts * acts, axis=-1, keepdims=True)
    return (acts * lax.rsqrt(mean_sq + NORM_EPS) * norm_scale.astype(jnp.float32)).astype(jnp.bfloat16)


def solution(mesh):
    def per_device(enc_out, norm_scale, w_key, w_value):
        normed = rms_norm(enc_out, norm_scale)
        gathered = lax.all_gather(normed, "tp", axis=1, tiled=True)
        key_cache = jnp.einsum("bsd,ldhk->lbshk", gathered, w_key, preferred_element_type=jnp.float32).astype(jnp.bfloat16)
        value_cache = jnp.einsum("bsd,ldhk->lbshk", gathered, w_value, preferred_element_type=jnp.float32).astype(jnp.bfloat16)
        return key_cache, value_cache

    weight_spec = P(None, None, "tp", None)
    cache_spec = P(None, "dp", None, "tp", None)
    return jax.shard_map(per_device, mesh=mesh, in_specs=(P("dp", "tp", None), P(None), weight_spec, weight_spec), out_specs=(cache_spec, cache_spec), check_vma=False)
```

profile of v0, /device:TPU:0, one launch (start us, length us, event | category | flops | bytes accessed | tf_op | source)
XLA Modules:
  0.0 577.8 jit_solution(16463841418124633277)
XLA Ops:
  7.2 0.0 all-gather.2.cloned.1.call-start
  7.2 5.1 fusion.14
  12.3 0.7 convert_element_type.22
  13.0 10.5 %fusion.16 = bf16[8,128,4096]{2,1,0:T(8,128)(2,1)} fusion(bf16[8,128,4096]{2,1,0:T(8,128)(2,1)} %param.4, f32[4096]{0:T(1024)S(1)} %convert_element_type.22, f32[8,128]{1,0:T(8,128)S(1)} %add_rsqrt_fusion), kind=kLoop, calls=%fused_computation.12 | loop fusion | flops 16777216 | bytes 16797696 | tf_op jit(solution)/shard_map/convert_element_type | solution.py:12
  23.5 0.0 all-gather.2.cloned.1.call-update
  23.5 203.2 %all-gather.2.cloned.1.call-done = bf16[8,512,4096]{2,1,0:T(8,128)(2,1)} async-done(((bf16[8,128,4096]{2,1,0:T(8,128)(2,1)}), bf16[8,512,4096]{2,1,0:T(8,128)(2,1)}) %all-gather.2.cloned.1.call-update) | async-done | bytes 33554448 | tf_op jit(solution)/shard_map/all_gather | solution.py:18
  226.8 149.0 %convert_bitcast_fusion.1 = bf16[4,8,512,16,64]{2,4,3,0,1:T(8,128)(2,1)} fusion(bf16[4,4096,16,64]{1,3,2,0:T(8,128)(2,1)} %param.6, bf16[8,512,4096]{2,1,0:T(8,128)(2,1)} %all-gather.2.cloned.1.call-done), kind=kOutput, calls=%fused_computation.7 | convolution fusion | flops 137455730688 | bytes 100663296 | tf_op jit(solution)/shard_map/bsd,ldhk->lbshk/dot_general | solution.py:19
  375.8 22.9 %copy.6 = bf16[4,8,512,16,64]{2,4,3,1,0:T(8,128)(2,1)} copy(bf16[4,8,512,16,64]{2,4,3,0,1:T(8,128)(2,1)} %convert_bitcast_fusion.1) | data formatting | bytes 67108864
  398.7 149.3 %convert_bitcast_fusion = bf16[4,8,512,16,64]{2,4,3,0,1:T(8,128)(2,1)} fusion(bf16[4,4096,16,64]{1,3,2,0:T(8,128)(2,1)} %param.7, bf16[8,512,4096]{2,1,0:T(8,128)(2,1)} %all-gather.2.cloned.1.call-done), kind=kOutput, calls=%fused_computation.6 | convolution fusion | flops 137455730688 | bytes 100663296 | tf_op jit(solution)/shard_map/bsd,ldhk->lbshk/dot_general | solution.py:20
  548.0 22.9 %copy.7 = bf16[4,8,512,16,64]{2,4,3,1,0:T(8,128)(2,1)} copy(bf16[4,8,512,16,64]{2,4,3,0,1:T(8,128)(2,1)} %convert_bitcast_fusion) | data formatting | bytes 67108864
  (1 shorter events, 0.0 us)
Async XLA Ops:
  7.2 219.6 %all-gather.2.cloned.1.call-start = ((), (), s32[]{:S(2)}) async-start(), calls=%async_computation | async-start | bytes 41943040 | tf_op jit(solution)/shard_map/all_gather | solution.py:18
Sparse Core Ops, SparseCore 0:
  23.7 203.0 all-gather.1
where the time goes:
time: 578 us
  matrix products  298 us (52%)
  waiting for transfers between devices  203 us (35%)
  local copies, waits for them, and re-layouts  45.8 us (8%)
  other arithmetic  16.3 us (3%)
  between operations  14 us (2%)
    all_gather x1, waiting for transfers between devices, per_device(): gathered = lax.all_gather(normed, 'tp', axis=1, tiled=True)  203 us
    dot_general x1, matrix products, per_device(): jnp.einsum('bsd,ldhk->lbshk', gathered, w_value, preferred_element_type=j...  149 us
    dot_general x1, matrix products, per_device(): jnp.einsum('bsd,ldhk->lbshk', gathered, w_key, preferred_element_type=jnp...  149 us
    unnamed x2, local copies, waits for them, and re-layouts  45.8 us
  transfers between devices with their start and end apart: 1, of which 1 were waited for; matrix products, arithmetic and copies ran while one was open for 0% of the time, Pallas kernels for 0%

commit v1 on v0

v1 whole, which is shorter than its diff:
```python
import functools

import jax
import jax.numpy as jnp
from jax import lax
from jax.experimental import pallas as pl
from jax.experimental.pallas import tpu as pltpu
from jax.sharding import PartitionSpec as P

NORM_EPS = 1e-6
LAYERS, D, ROWS = 4, 4096, 1024
TM = 512
STEPS = LAYERS * ROWS // TM
CH = 4
SEQ = 2
TOK = 128
BF16 = jnp.bfloat16
F32 = jnp.float32
VMEM = pltpu.VMEM
HBM = pltpu.HBM
DMA = pltpu.SemaphoreType.DMA

UNROLL = {"own_rest": 4, "near_a": 4, "near_b": 4, "far_a1": 4, "far_a2": 1, "far_b": 4}


def normed_rows(x, scale):
    acts = x.astype(F32)
    mean_sq = jnp.mean(acts * acts, axis=-1, keepdims=True)
    return (acts * lax.rsqrt(mean_sq + NORM_EPS) * scale).astype(BF16)


def w_copies(wk, wv, ring, wsem, step):
    return [pltpu.make_async_copy(w.at[step], ring.at[step % 2, i], wsem.at[i]) for i, w in enumerate((wk, wv))]


def out_copies(ok, ov, obuf, osem, step, slot, where, row0, chunks):
    copies = []
    row = pl.multiple_of((step % 2) * TM, TM)
    for c in chunks:
        lane = pl.multiple_of(where[row0 * CH + c] * TOK, TOK)
        first = where[(row0 + 1) * CH + c]
        for i, o in enumerate((ok, ov)):
            dst = o.at[step // 2, pl.ds(first, SEQ), pl.ds(row, TM), pl.ds(lane, TOK)]
            copies.append(pltpu.make_async_copy(obuf.at[slot, i, c], dst, osem.at[i * CH + c]))
    return copies


def project(ring, slot, y, obuf, c):
    tokens = y[c].reshape(SEQ * TOK, D)
    for i in range(2):
        out = lax.dot_general(ring[slot, i], tokens, (((1,), (1,)), ((), ())), preferred_element_type=F32).astype(BF16)
        for s in range(SEQ):
            obuf[slot, i, c, s] = out[:, s * TOK:(s + 1) * TOK]


def first_body(where, x_hbm, scale_ref, wk, wv, ok, ov, s0, s1, s2, s3, ring, obuf, y, xbuf, xsem, wsem, nsem, ssem):
    sends = (s0, s1, s2, s3)
    xcp = [pltpu.make_async_copy(x_hbm.at[pl.ds(c * SEQ, SEQ)], xbuf.at[c], xsem.at[c]) for c in range(CH)]
    scp = [pltpu.make_async_copy(y.at[c], sends[c], ssem.at[c]) for c in range(CH)]
    wcp = w_copies(wk, wv, ring, wsem, 0)
    ncp = w_copies(wk, wv, ring, nsem, 1)
    for cp in (xcp[0], wcp[0], xcp[1], wcp[1], xcp[2], xcp[3], *ncp):
        cp.start()
    scale = scale_ref[...].astype(F32)

    def norm_chunk(c):
        for s in range(SEQ):
            for r in range(0, TOK, 16):
                y[c, s, r:r + 16] = normed_rows(xbuf[c, s, r:r + 16], scale)

    xcp[0].wait()
    norm_chunk(0)
    wcp[0].wait()
    wcp[1].wait()
    for c in range(CH):
        scp[c].start()
        if c + 1 < CH:
            xcp[c + 1].wait()
            norm_chunk(c + 1)
        project(ring, 0, y, obuf, c)
    for cp in (*ncp, *scp):
        cp.wait()


def rest_body(s0, n, spot, prev, load, last, unroll, *refs):
    it = iter(refs)
    where = next(it)
    srcs = [next(it) for _ in range(CH)] if load else []
    wk, wv = next(it), next(it)
    for _ in range(5):
        next(it)
    ok, ov, ring, obuf, y, wsem, osem, ysem = it
    for c in range(len(srcs)):
        pltpu.make_async_copy(srcs[c], y.at[c], ysem.at[c]).start()

    def step(t, first):
        s = s0 + t
        slot = s % 2
        row0 = jnp.where(t == 0, 2 * prev, 2 * spot)
        leaving = out_copies(ok, ov, obuf, osem, (s + STEPS - 1) % STEPS, 1 - slot, where, row0, range(CH))
        for cp in leaving:
            cp.start()
        arriving = w_copies(wk, wv, ring, wsem, (s + 1) % STEPS)
        more = t + 1 < n if last else True

        def each(op):
            def run():
                for cp in arriving:
                    getattr(cp, op)()

            if last:
                pl.when(more)(run)
            else:
                run()

        each("start")
        if first:
            def chunk(c, _):
                pltpu.make_async_copy(srcs[0], y.at[c], ysem.at[c]).wait()
                project(ring, slot, y, obuf, c)
                return 0

            lax.fori_loop(0, CH, chunk, 0)
        elif unroll < CH:
            def group(g, _):
                for u in range(unroll):
                    project(ring, slot, y, obuf, g * unroll + u)
                return 0

            lax.fori_loop(0, CH // unroll, group, 0)
        else:
            for c in range(CH):
                project(ring, slot, y, obuf, c)
        for cp in leaving:
            cp.wait()
        each("wait")

    if load:
        step(jnp.int32(0), True)

    def body(t, _):
        step(t, False)
        return 0

    lax.fori_loop(1 if load else 0, n, body, 0)
    if last:
        end = out_copies(ok, ov, obuf, osem, s0 + n - 1, (s0 + n - 1) % 2, where, 2 * spot, range(CH))
        for cp in end:
            cp.start()
        for cp in end:
            cp.wait()


ANY_SPEC = pl.BlockSpec(memory_space=pl.ANY)
SMEM_SPEC = pl.BlockSpec(memory_space=pltpu.SMEM)
VMEM_SPEC = pl.BlockSpec(memory_space=VMEM)
CHUNK = (SEQ, TOK, D)
CACHE = (LAYERS, 4 * SEQ, ROWS, 4 * TOK)
RING = (2, 2, TM, D)
OBUF = (2, 2, CH, SEQ, TM, TOK)


def hbm(a):
    return pltpu.with_memory_space_constraint(a, HBM)


def cost(n):
    return pl.CostEstimate(flops=n * 2 * 2 * TM * D * CH * SEQ * TOK, bytes_accessed=n * 2 * TM * D * 2, transcendentals=0)


TOKENS = (CH,) + CHUNK


def first_call(where, x, scale, wk, wv):
    return pl.pallas_call(
        first_body,
        in_specs=[SMEM_SPEC, ANY_SPEC, VMEM_SPEC, ANY_SPEC, ANY_SPEC],
        out_specs=[ANY_SPEC] * (2 + CH) + [VMEM_SPEC] * 3,
        out_shape=[HBM(CACHE, BF16)] * 2 + [HBM(CHUNK, BF16)] * CH + [VMEM(RING, BF16), VMEM(OBUF, BF16), VMEM(TOKENS, BF16)],
        scratch_shapes=[VMEM(TOKENS, BF16), DMA((CH,)), DMA((2,)), DMA((2,)), DMA((CH,))],
        cost_estimate=cost(1), name="own_first",
        compiler_params=pltpu.CompilerParams(vmem_limit_bytes=35 * 2**20),
    )(where, hbm(x), scale, hbm(wk), hbm(wv))


def rest_call(s0, n, spot, prev, where, srcs, state, wk, wv, last=False, unroll=CH):
    held = [pltpu.with_memory_space_constraint(a, VMEM) for a in state[2:]]
    args = [where, *map(hbm, srcs), hbm(wk), hbm(wv), *map(hbm, state[:2]), *held]
    k = len(args) - len(state)
    return pl.pallas_call(
        functools.partial(rest_body, s0, n, spot, prev, bool(srcs), last, unroll),
        in_specs=[SMEM_SPEC] + [ANY_SPEC] * (k + 1) + [VMEM_SPEC] * 3,
        out_specs=[ANY_SPEC] * 2 + [VMEM_SPEC] * 3,
        out_shape=[HBM(CACHE, BF16)] * 2 + [VMEM(RING, BF16), VMEM(OBUF, BF16), VMEM(TOKENS, BF16)],
        input_output_aliases={k + i: i for i in range(len(state))},
        scratch_shapes=[DMA((2,)), DMA((2 * CH,)), DMA((CH,))],
        cost_estimate=cost(n),
        compiler_params=pltpu.CompilerParams(vmem_limit_bytes=35 * 2**20),
    )(*args)


def solution(mesh):
    def per_device(enc_out, norm_scale, w_key, w_value):
        wk, wv = (jnp.transpose(w, (0, 2, 3, 1)).reshape(STEPS, TM, D) for w in (w_key, w_value))
        me = lax.axis_index("tp").astype(jnp.int32)
        sib = [(i, i ^ 1) for i in range(4)]
        far = [(i, i ^ 2) for i in range(4)]
        flips = ((0, 0, 0, 0), (1, 1, 1, 1), (2, 2, 3, 3), (2, 2, 3, 3))
        firsts = ((0, 2, 4, 6), (0, 2, 4, 6), (0, 2, 0, 2), (4, 6, 4, 6))
        flip = jnp.array([f for a in flips for f in (*a, 0, 0, 0, 0)], jnp.int32)
        first = jnp.array([f for a in firsts for f in (0, 0, 0, 0, *a)], jnp.int32)
        here = jnp.array([1, 1, 1, 1, 0, 0, 0, 0] * 4, jnp.int32)
        where = (me ^ flip) * here + first

        r = first_call(where, enc_out, norm_scale.reshape(1, D), wk, wv)
        own, state = r[2:6], (*r[:2], *r[6:])
        direct, near, passed = [None] * 4, [None] * 4, [None] * 4
        for c in range(CH):
            direct[c] = lax.ppermute(own[c], "tp", far)
            near[c] = lax.ppermute(own[c], "tp", sib)
        for c in range(CH):
            passed[c] = lax.ppermute(direct[c], "tp", sib)
        ya = [direct[0], direct[1], passed[0], passed[1]]
        yb = [direct[2], direct[3], passed[2], passed[3]]
        plan = (
            ("own_rest", 1, 7, 0, 0, []),
            ("near_a", 0, 4, 1, 0, near),
            ("near_b", 4, 4, 1, 1, []),
            ("far_a1", 0, 6, 2, 1, ya),
            ("far_a2", 6, 2, 2, 2, []),
            ("far_b", 0, 8, 3, 2, yb),
        )
        for name, s0, n, spot, prev, srcs in plan:
            state = rest_call(s0, n, spot, prev, where, srcs, state, wk, wv, last=name == "far_b", unroll=UNROLL[name])
        return tuple(jnp.transpose(o.reshape(LAYERS, 8, 16, 64, 512), (0, 1, 4, 2, 3)) for o in state[:2])

    weight_spec = P(None, None, "tp", None)
    cache_spec = P(None, "dp", None, "tp", None)
    return jax.shard_map(per_device, mesh=mesh, in_specs=(P("dp", "tp", None), P(None), weight_spec, weight_spec), out_specs=(cache_spec, cache_spec), check_vma=False)
```

time: 578 us -> 443 us (0.77); the launches traced: 578 us -> 435 us
  Pallas kernels: 0 us -> 310 us
  matrix products: 298 us -> 0 us
  waiting for transfers between devices: 203 us -> 109 us
  local copies, waits for them, and re-layouts: 45.8 us -> 1.32 us
  other arithmetic: 16.3 us -> 1.26 us
  between operations: 14 us -> 1.21 us
  starting transfers between devices: 0.04 us -> 12.6 us
    pallas_call x0 -> x7, Pallas kernels: none -> 310 us  [the longest x6 293 us: rest_call(): pl.pallas_call(functools.partial(rest_body, s0, n, spot, prev, bool(srcs)...]
    dot_general x2 -> x0, matrix products: 298 us -> none  [the longest x1 149 us: per_device(): jnp.einsum('bsd,ldhk->lbshk', gathered, w_value, preferred_element_type=j...]
    all_gather x1 -> x0, waiting for transfers between devices: 203 us -> none  [per_device(): gathered = lax.all_gather(normed, 'tp', axis=1, tiled=True)]
    ppermute x0 -> x12, waiting for transfers between devices: none -> 109 us  [the longest x4 108 us: per_device(): direct[c] = lax.ppermute(own[c], 'tp', far)]
    unnamed x2 -> x6, local copies, waits for them, and re-layouts: 45.8 us -> 0.01 us
    ppermute x0 -> x12, starting transfers between devices: none -> 12.6 us  [the longest x4 11.1 us: per_device(): direct[c] = lax.ppermute(own[c], 'tp', far)]
    convert_element_type x2 -> x0, other arithmetic: 11.2 us -> none  [the longest x1 10.5 us: rms_norm(): (acts * lax.rsqrt(mean_sq + NORM_EPS) * norm_scale.astype(jnp.float32)).a...]
  transfers between devices with their start and end apart: 1 -> 12, of which waited for: 1 -> 6; matrix products, arithmetic and copies ran while one was open for 0% -> 0% of each run, Pallas kernels for 0% -> 50%
where the time goes in v1:
time: 443 us; the launch traced here: 435 us
  Pallas kernels  310 us (70%)
  waiting for transfers between devices  109 us (25%)
  starting transfers between devices  12.6 us (3%)
    pallas_call x6, Pallas kernels, rest_call(): pl.pallas_call(functools.partial(rest_body, s0, n, spot, prev, bool(srcs)...  293 us
    ppermute x4, waiting for transfers between devices, per_device(): direct[c] = lax.ppermute(own[c], 'tp', far)  108 us
    pallas_call x1, Pallas kernels, first_call(): pl.pallas_call(first_body, in_specs=[SMEM_SPEC, ANY_SPEC, VMEM_SPEC, ANY_...  16.9 us
    ppermute x4, starting transfers between devices, per_device(): direct[c] = lax.ppermute(own[c], 'tp', far)  11.1 us
  transfers between devices with their start and end apart: 12, of which 6 were waited for; matrix products, arithmetic and copies ran while one was open for 0% of the time, Pallas kernels for 50%

profile of v1, /device:TPU:0, one launch (start us, length us, event | category | flops | bytes accessed | tf_op | source)
XLA Modules:
  0.0 435.3 jit_solution(4033633155964982369)
XLA Ops:
  0.6 1.3 reshape.19.scale_ref
  1.9 1.3 multiply_add_fusion.where.refs_0_
  3.2 16.9 %own_first.1 = (bf16[4,8,1024,512]{3,2,1,0:T(8,128)(2,1)}, bf16[4,8,1024,512]{3,2,1,0:T(8,128)(2,1)}, bf16[2,128,4096]{2,1,0:T(8,128)(2,1)}, bf16[2,128,4096]{2,...) custom-call(s32[32]{0:T(128)} %multiply_add_fusion.where.refs_0_, ...), custom_call_target="tpu_custom_call" | custom-call | flops 8589934592 | bytes 8388608 | tf_op jit(solution)/shard_map/own_first/pallas_call | solution.py:175
  20.1 0.8 collective-permute-start.10
  20.8 0.0 collective-permute-start.11
  20.9 0.5 collective-permute-start.8
  21.3 2.5 collective-permute-start.4
  23.9 0.2 collective-permute-start.9
  24.0 0.8 collective-permute-done.10.refs_3_
  24.8 0.0 copy-start
  24.8 2.9 collective-permute-start.5
  27.7 0.1 collective-permute-done.11.refs_4_
  27.8 0.0 copy-start.1
  27.8 2.9 collective-permute-start
  30.7 0.1 collective-permute-done.8.refs_1_
  30.8 0.0 copy-start.2
  30.8 2.9 collective-permute-start.1
  33.7 0.0 copy-done
  33.7 0.0 copy-done.1
  33.7 0.0 copy-done.2
  33.7 63.7 %shard_map.86 = (bf16[4,8,1024,512]{3,2,1,0:T(8,128)(2,1)}, bf16[4,8,1024,512]{3,2,1,0:T(8,128)(2,1)}, bf16[2,2,512,4096]{3,2,1,0:T(8,128)(2,1)S(1)}, bf16[2,2,4...) custom-call(s32[32]{0:T(128)} %multiply_add_fusion.where.refs_0_, ...), custom_call_target="tpu_custom_call", output_to_operand_aliasing={{0}: (3, {}), {1}: (4, {}), {2}: (5, {}), {3}: (6, {}), {4}... | custom-call | flops 60129542144 | bytes 58720256 | tf_op jit(solution)/shard_map/pallas_call | solution.py:190
  97.4 0.0 collective-permute-done.4.refs_1_
  97.4 0.0 collective-permute-start.6
  97.4 18.2 %collective-permute-done.5.refs_2_ = bf16[2,128,4096]{2,1,0:T(8,128)(2,1)} collective-permute-done((bf16[2,128,4096]{2,1,0:T(8,128)(2,1)}, bf16[2,128,4096]{2,1,0:T(8,128)(2,1)}, u32[]{:S(2)}, u32[]{:S(2)}) %collective-permute-start.5) | collective-permute-done | bytes 2097184 | tf_op jit(solution)/shard_map/ppermute | solution.py:219
  115.6 0.0 collective-permute-start.7
  115.6 44.9 %collective-permute-done.refs_1_ = bf16[2,128,4096]{2,1,0:T(8,128)(2,1)} collective-permute-done((bf16[2,128,4096]{2,1,0:T(8,128)(2,1)}, bf16[2,128,4096]{2,1,0:T(8,128)(2,1)}, u32[]{:S(2)}, u32[]{:S(2)}) %collective-permute-start) | collective-permute-done | bytes 2097184 | tf_op jit(solution)/shard_map/ppermute | solution.py:219
  160.5 0.0 collective-permute-start.2
  160.5 44.7 %collective-permute-done.1.refs_2_ = bf16[2,128,4096]{2,1,0:T(8,128)(2,1)} collective-permute-done((bf16[2,128,4096]{2,1,0:T(8,128)(2,1)}, bf16[2,128,4096]{2,1,0:T(8,128)(2,1)}, u32[]{:S(2)}, u32[]{:S(2)}) %collective-permute-start.1) | collective-permute-done | bytes 2097184 | tf_op jit(solution)/shard_map/ppermute | solution.py:219
  205.2 0.0 collective-permute-start.3
  205.3 0.0 collective-permute-done.9.refs_2_
  205.3 39.5 %shard_map.87 = (bf16[4,8,1024,512]{3,2,1,0:T(8,128)(2,1)}, bf16[4,8,1024,512]{3,2,1,0:T(8,128)(2,1)}, bf16[2,2,512,4096]{3,2,1,0:T(8,128)(2,1)S(1)}, bf16[2,2,4...) custom-call(s32[32]{0:T(128)} %multiply_add_fusion.where.refs_0_, ...), custom_call_target="tpu_custom_call", output_to_operand_aliasing={{0}: (7, {}), {1}: (8, {}), {2}: (9, {}), {3}: (10, {}), {4... | custom-call | flops 34359738368 | bytes 33554432 | tf_op jit(solution)/shard_map/pallas_call | solution.py:190
  244.8 36.4 %shard_map.88 = (bf16[4,8,1024,512]{3,2,1,0:T(8,128)(2,1)}, bf16[4,8,1024,512]{3,2,1,0:T(8,128)(2,1)}, bf16[2,2,512,4096]{3,2,1,0:T(8,128)(2,1)S(1)}, bf16[2,2,4...) custom-call(s32[32]{0:T(128)} %multiply_add_fusion.where.refs_0_, ...), custom_call_target="tpu_custom_call", output_to_operand_aliasing={{0}: (3, {}), {1}: (4, {}), {2}: (5, {}), {3}: (6, {}), {4}... | custom-call | flops 34359738368 | bytes 33554432 | tf_op jit(solution)/shard_map/pallas_call | solution.py:190
  281.2 0.0 collective-permute-done.6.refs_3_
  281.2 0.0 collective-permute-done.7.refs_4_
  281.2 57.2 %shard_map.89 = (bf16[4,8,1024,512]{3,2,1,0:T(8,128)(2,1)}, bf16[4,8,1024,512]{3,2,1,0:T(8,128)(2,1)}, bf16[2,2,512,4096]{3,2,1,0:T(8,128)(2,1)S(1)}, bf16[2,2,4...) custom-call(s32[32]{0:T(128)} %multiply_add_fusion.where.refs_0_, ...), custom_call_target="tpu_custom_call", output_to_operand_aliasing={{0}: (7, {}), {1}: (8, {}), {2}: (9, {}), {3}: (10, {}), {4... | custom-call | flops 51539607552 | bytes 50331648 | tf_op jit(solution)/shard_map/pallas_call | solution.py:190
  338.4 19.9 %shard_map.90 = (bf16[4,8,1024,512]{3,2,1,0:T(8,128)(2,1)}, bf16[4,8,1024,512]{3,2,1,0:T(8,128)(2,1)}, bf16[2,2,512,4096]{3,2,1,0:T(8,128)(2,1)S(1)}, bf16[2,2,4...) custom-call(s32[32]{0:T(128)} %multiply_add_fusion.where.refs_0_, ...), custom_call_target="tpu_custom_call", output_to_operand_aliasing={{0}: (3, {}), {1}: (4, {}), {2}: (5, {}), {3}: (6, {}), {4}... | custom-call | flops 17179869184 | bytes 16777216 | tf_op jit(solution)/shard_map/pallas_call | solution.py:190
  358.3 0.0 collective-permute-done.2.refs_3_
  358.3 0.0 collective-permute-done.3.refs_4_
  358.3 76.5 %shard_map.91 = (bf16[4,8,1024,512]{3,2,1,0:T(8,128)(2,1)}, bf16[4,8,1024,512]{3,2,1,0:T(8,128)(2,1)}, bf16[2,2,512,4096]{3,2,1,0:T(8,128)(2,1)S(1)}, bf16[2,2,4...) custom-call(s32[32]{0:T(128)} %multiply_add_fusion.where.refs_0_, ...), custom_call_target="tpu_custom_call", output_to_operand_aliasing={{0}: (7, {}), {1}: (8, {}), {2}: (9, {}), {3}: (10, {}), {4... | custom-call | flops 68719476736 | bytes 67108864 | tf_op jit(solution)/shard_map/pallas_call | solution.py:190
Async XLA Ops:
  20.1 4.8 %collective-permute-start.10 = (bf16[2,128,4096]{2,1,0:T(8,128)(2,1)}, bf16[2,128,4096]{2,1,0:T(8,128)(2,1)S(1)}, u32[]{:S(2)}, u32[]{:S(2)}) collective-permute-start(bf16[2,128,4096]{2,1,0:T(8,128)(2,1)} %get-tuple-element.38), channel_id=1, source_target_pairs={{0,1},{1,0},{2,3},{3,2},{4,5},{5,4},{6,7},{7,6},{8,9},{9,8},{10,11... | collective-permute-start | bytes 6291464 | tf_op jit(solution)/shard_map/ppermute | solution.py:220
  20.8 7.0 %collective-permute-start.11 = (bf16[2,128,4096]{2,1,0:T(8,128)(2,1)}, bf16[2,128,4096]{2,1,0:T(8,128)(2,1)S(1)}, u32[]{:S(2)}, u32[]{:S(2)}) collective-permute-start(bf16[2,128,4096]{2,1,0:T(8,128)(2,1)} %get-tuple-element.39), channel_id=1, source_target_pairs={{0,1},{1,0},{2,3},{3,2},{4,5},{5,4},{6,7},{7,6},{8,9},{9,8},{10,11... | collective-permute-start | bytes 6291464 | tf_op jit(solution)/shard_map/ppermute | solution.py:220
  20.9 9.9 %collective-permute-start.8 = (bf16[2,128,4096]{2,1,0:T(8,128)(2,1)}, bf16[2,128,4096]{2,1,0:T(8,128)(2,1)S(1)}, u32[]{:S(2)}, u32[]{:S(2)}) collective-permute-start(bf16[2,128,4096]{2,1,0:T(8,128)(2,1)} %get-tuple-element.40), channel_id=1, source_target_pairs={{0,1},{1,0},{2,3},{3,2},{4,5},{5,4},{6,7},{7,6},{8,9},{9,8},{10,11... | collective-permute-start | bytes 6291464 | tf_op jit(solution)/shard_map/ppermute | solution.py:220
  21.3 76.1 %collective-permute-start.4 = (bf16[2,128,4096]{2,1,0:T(8,128)(2,1)}, bf16[2,128,4096]{2,1,0:T(8,128)(2,1)}, u32[]{:S(2)}, u32[]{:S(2)}) collective-permute-start(bf16[2,128,4096]{2,1,0:T(8,128)(2,1)} %get-tuple-element.40), channel_id=1, source_target_pairs={{0,2},{1,3},{2,0},{3,1},{4,6},{5,7},{6,4},{7,5},{8,10},{9,11},{10,... | collective-permute-start | bytes 6291464 | tf_op jit(solution)/shard_map/ppermute | solution.py:219
  23.9 181.4 %collective-permute-start.9 = (bf16[2,128,4096]{2,1,0:T(8,128)(2,1)}, bf16[2,128,4096]{2,1,0:T(8,128)(2,1)}, u32[]{:S(2)}, u32[]{:S(2)}) collective-permute-start(bf16[2,128,4096]{2,1,0:T(8,128)(2,1)} %get-tuple-element.41), channel_id=1, source_target_pairs={{0,1},{1,0},{2,3},{3,2},{4,5},{5,4},{6,7},{7,6},{8,9},{9,8},{10,11... | collective-permute-start | bytes 6291464 | tf_op jit(solution)/shard_map/ppermute | solution.py:220
  24.8 8.9 %copy-start = (bf16[2,128,4096]{2,1,0:T(8,128)(2,1)}, bf16[2,128,4096]{2,1,0:T(8,128)(2,1)S(1)}, u32[]{:S(2)}) copy-start(bf16[2,128,4096]{2,1,0:T(8,128)(2,1)S(1)} %collective-permute-done.10.refs_3_) | copy-start | bytes 6291460
  24.8 90.8 %collective-permute-start.5 = (bf16[2,128,4096]{2,1,0:T(8,128)(2,1)}, bf16[2,128,4096]{2,1,0:T(8,128)(2,1)}, u32[]{:S(2)}, u32[]{:S(2)}) collective-permute-start(bf16[2,128,4096]{2,1,0:T(8,128)(2,1)} %get-tuple-element.41), channel_id=1, source_target_pairs={{0,2},{1,3},{2,0},{3,1},{4,6},{5,7},{6,4},{7,5},{8,10},{9,11},{10,... | collective-permute-start | bytes 6291464 | tf_op jit(solution)/shard_map/ppermute | solution.py:219
  27.8 5.9 %copy-start.1 = (bf16[2,128,4096]{2,1,0:T(8,128)(2,1)}, bf16[2,128,4096]{2,1,0:T(8,128)(2,1)S(1)}, u32[]{:S(2)}) copy-start(bf16[2,128,4096]{2,1,0:T(8,128)(2,1)S(1)} %collective-permute-done.11.refs_4_) | copy-start | bytes 6291460
  27.8 132.7 %collective-permute-start = (bf16[2,128,4096]{2,1,0:T(8,128)(2,1)}, bf16[2,128,4096]{2,1,0:T(8,128)(2,1)}, u32[]{:S(2)}, u32[]{:S(2)}) collective-permute-start(bf16[2,128,4096]{2,1,0:T(8,128)(2,1)} %get-tuple-element.38), channel_id=1, source_target_pairs={{0,2},{1,3},{2,0},{3,1},{4,6},{5,7},{6,4},{7,5},{8,10},{9,11},{10,... | collective-permute-start | bytes 6291464 | tf_op jit(solution)/shard_map/ppermute | solution.py:219
  30.8 2.9 copy-start.2
  30.8 174.4 %collective-permute-start.1 = (bf16[2,128,4096]{2,1,0:T(8,128)(2,1)}, bf16[2,128,4096]{2,1,0:T(8,128)(2,1)}, u32[]{:S(2)}, u32[]{:S(2)}) collective-permute-start(bf16[2,128,4096]{2,1,0:T(8,128)(2,1)} %get-tuple-element.39), channel_id=1, source_target_pairs={{0,2},{1,3},{2,0},{3,1},{4,6},{5,7},{6,4},{7,5},{8,10},{9,11},{10,... | collective-permute-start | bytes 6291464 | tf_op jit(solution)/shard_map/ppermute | solution.py:219
  97.4 183.8 %collective-permute-start.6 = (bf16[2,128,4096]{2,1,0:T(8,128)(2,1)}, bf16[2,128,4096]{2,1,0:T(8,128)(2,1)}, u32[]{:S(2)}, u32[]{:S(2)}) collective-permute-start(bf16[2,128,4096]{2,1,0:T(8,128)(2,1)} %collective-permute-done.4.refs_1_), channel_id=1, source_target_pairs={{0,1},{1,0},{2,3},{3,2},{4,5},{5,4},{6,7},{7,6},{8,9},{9,8},{10,11... | collective-permute-start | bytes 6291464 | tf_op jit(solution)/shard_map/ppermute | solution.py:222
  115.6 165.6 %collective-permute-start.7 = (bf16[2,128,4096]{2,1,0:T(8,128)(2,1)}, bf16[2,128,4096]{2,1,0:T(8,128)(2,1)}, u32[]{:S(2)}, u32[]{:S(2)}) collective-permute-start(bf16[2,128,4096]{2,1,0:T(8,128)(2,1)} %collective-permute-done.5.refs_2_), channel_id=1, source_target_pairs={{0,1},{1,0},{2,3},{3,2},{4,5},{5,4},{6,7},{7,6},{8,9},{9,8},{10,11... | collective-permute-start | bytes 6291464 | tf_op jit(solution)/shard_map/ppermute | solution.py:222
  160.5 197.8 %collective-permute-start.2 = (bf16[2,128,4096]{2,1,0:T(8,128)(2,1)}, bf16[2,128,4096]{2,1,0:T(8,128)(2,1)}, u32[]{:S(2)}, u32[]{:S(2)}) collective-permute-start(bf16[2,128,4096]{2,1,0:T(8,128)(2,1)} %collective-permute-done.refs_1_), channel_id=1, source_target_pairs={{0,1},{1,0},{2,3},{3,2},{4,5},{5,4},{6,7},{7,6},{8,9},{9,8},{10,11... | collective-permute-start | bytes 6291464 | tf_op jit(solution)/shard_map/ppermute | solution.py:222
  205.2 153.1 %collective-permute-start.3 = (bf16[2,128,4096]{2,1,0:T(8,128)(2,1)}, bf16[2,128,4096]{2,1,0:T(8,128)(2,1)}, u32[]{:S(2)}, u32[]{:S(2)}) collective-permute-start(bf16[2,128,4096]{2,1,0:T(8,128)(2,1)} %collective-permute-done.1.refs_2_), channel_id=1, source_target_pairs={{0,1},{1,0},{2,3},{3,2},{4,5},{5,4},{6,7},{7,6},{8,9},{9,8},{10,11... | collective-permute-start | bytes 6291464 | tf_op jit(solution)/shard_map/ppermute | solution.py:222
